TPU v7x, 32 devices: a whole 2x2x4 slice. The times are simulated.
32 devices in a mesh: px: 2 (over core), py: 4 (over z), ta: 4 (over y, x).
Axes of the slice: x: 2, y: 2, z: 4, core: 2. Of those that a mesh axis runs over, the one named last changes fastest.
Arguments:
- snapshots: bfloat16 [384, 5, 65536], P('ta', None, ('px', 'py')), may hold values from -6 to 6
- quad_weights: float32 [65536], P(('px', 'py')), may hold values from 1 to 10
- spectral_indices: int32 [32], replicated, may hold values from 0 to 127
Outputs:
- spectra: float32 [32, 2, 2, 5, 65536], P('ta', None, None, None, ('px', 'py'))
- gram: float32 [32, 2, 2, 2], P('ta')
All inputs are finite; a program needn't handle non-finite values.
Results may differ from a plain program's by a relative error of at most 0.0042.
Values may be sent and summed in bfloat16 or wider, within the bound.
A program may use at most 128 MiB of HBM per device.

v0:
```python
import math

import jax
import jax.numpy as jnp
from jax import lax
from jax.sharding import PartitionSpec as P

VARS = 5
BLK = 256
HOP = 128
SEGMENT_NUMBER = 2
RETAINED_MODES = 32


def make_rotation_multipliers(spectral_indices, temporal_locations):
    segment_beginnings = jnp.arange(SEGMENT_NUMBER, dtype=jnp.int32) * HOP
    segment_shifts = temporal_locations[None, :] - segment_beginnings[:, None]
    inside = (segment_shifts >= 0) & (segment_shifts < BLK)
    window = 0.5 - 0.5 * jnp.cos(2.0 * math.pi * segment_shifts.astype(jnp.float32) / BLK)
    window = jnp.where(inside, window, jnp.float32(0.0)) / jnp.sqrt(jnp.float32(3.0 * BLK / 8.0))
    phases = jnp.mod(spectral_indices[:, None, None] * segment_shifts[None, :, :], BLK)
    angles = 2.0 * math.pi * phases.astype(jnp.float32) / BLK
    real_part = jnp.cos(angles) * window[None]
    imag_part = -jnp.sin(angles) * window[None]
    gathered_segments = jnp.stack([real_part, imag_part], axis=2)
    return gathered_segments.reshape(
        RETAINED_MODES * SEGMENT_NUMBER * 2, temporal_locations.shape[0]
    ).astype(jnp.bfloat16)


def gram_terms(spectra):
    flat = spectra.reshape(spectra.shape[0], 2 * SEGMENT_NUMBER, -1)
    inner = jnp.einsum("fam,fbm->fab", flat, flat, precision=lax.Precision.HIGHEST)
    inner = inner.reshape(spectra.shape[0], SEGMENT_NUMBER, 2, SEGMENT_NUMBER, 2)
    real_part = inner[:, :, 0, :, 0] + inner[:, :, 1, :, 1]
    imag_part = inner[:, :, 0, :, 1] - inner[:, :, 1, :, 0]
    return jnp.stack([real_part, imag_part], axis=-1)


def on_device(snapshots, quad_weights, spectral_indices):
    record_length = snapshots.shape[0]
    point_count = snapshots.shape[2]
    groups = lax.axis_size("ta")
    temporal_locations = lax.axis_index("ta") * record_length + jnp.arange(
        record_length, dtype=jnp.int32
    )
    rotation_multipliers = make_rotation_multipliers(spectral_indices, temporal_locations)
    flat_snapshots = snapshots.reshape(record_length, VARS * point_count)
    raw = lax.psum_scatter(
        jnp.dot(rotation_multipliers, flat_snapshots, preferred_element_type=jnp.float32),
        "ta",
        scatter_dimension=0,
        tiled=True,
    )
    raw = raw.reshape(RETAINED_MODES // groups, SEGMENT_NUMBER, 2, VARS, point_count)
    spectra = raw * jnp.sqrt(quad_weights)
    summed = lax.psum(gram_terms(spectra), ("px", "py"))
    total_points = point_count * lax.axis_size("px") * lax.axis_size("py")
    gram = summed / jnp.float32(total_points * VARS)
    return (spectra, gram)


def solution(mesh):
    return jax.shard_map(
        on_device,
        mesh=mesh,
        in_specs=(P("ta", None, ("px", "py")), P(("px", "py")), P()),
        out_specs=(P("ta", None, None, None, ("px", "py")), P("ta", None, None, None)),
        check_vma=False,
    )
```

profile of v0, /device:TPU:0, one launch (start us, length us, event | category | flops | bytes accessed | tf_op | source)
XLA Modules:
  0.0 306.3 jit_solution(16101970219021868528)
XLA Ops:
  7.2 0.0 reduce-scatter.2.cloned.1.call-start
  7.2 0.1 broadcast_subtract_fusion
  7.3 0.1 fusion.6
  7.4 0.9 multiply_convert_fusion.1
  8.4 12.7 %copy.17 = bf16[96,5,8192]{0,2,1:T(8,128)(2,1)} copy(bf16[96,5,8192]{2,0,1:T(8,128)(2,1)} %param.3) | data formatting | bytes 15728640 | tf_op args[0]
  21.1 13.8 %fusion.7 = f32[128,40960]{1,0:T(8,128)} fusion(bf16[128,96]{1,0:T(8,128)(2,1)S(1)} %bitcast.8, bf16[96,40960]{0,1:T(8,128)(2,1)} %bitcast.7), kind=kOutput, calls=%fused_computation.24 | convolution fusion | flops 1006632960 | bytes 28860416 | tf_op jit(solution)/shard_map/dot_general | solution.py:50
  34.9 0.0 copy-start
  34.9 0.0 reduce-scatter.2.cloned.1.call-update
  35.0 0.7 copy-done
  35.7 0.1 mul.103
  35.8 189.7 %reduce-scatter.2.cloned.1.call-done = f32[32,40960]{1,0:T(8,128)} async-done(((f32[128,40960]{1,0:T(8,128)}), f32[32,40960]{1,0:T(8,128)}) %reduce-scatter.2.cloned.1.call-update) | async-done | bytes 5242896 | tf_op jit(solution)/shard_map/reduce_scatter | solution.py:49
  225.6 5.8 %reshape.194 = f32[8,4,40960]{2,1,0:T(4,128)} reshape(f32[32,40960]{1,0:T(8,128)} %reduce-scatter.2.cloned.1.call-done) | data formatting | bytes 10485760 | tf_op jit(solution)/shard_map/reshape | solution.py:55
  231.4 25.9 %fusion = f32[8,4,4]{2,1,0:T(4,128)S(1)} fusion(f32[8,4,40960]{2,1,0:T(4,128)} %reshape.194, f32[40960]{0:T(1024)S(1)} %mul.103), kind=kOutput, calls=%fused_computation | convolution fusion | flops 64225280 | bytes 5407232 | tf_op jit(solution)/shard_map/fam,fbm->fab/dot_general | solution.py:33
  257.3 0.1 copy.18
  257.5 16.5 %psum.7 = f32[8,2,2,2]{0,2,3,1:T(2,128)S(1)} all-reduce(f32[8,2,2,2]{0,2,3,1:T(2,128)S(1)} %pad_maximum_fusion.1), channel_id=1, replica_groups=mesh['px'=2,'py'=4,'ta'=4] {'px','py'}, use_global_device_ids=true, to_apply=%region_1.2 | all-reduce | flops 64 | bytes 512 | tf_op jit(solution)/shard_map/psum | solution.py:57
  274.0 0.6 copy.20
  274.6 7.3 %reshape.193 = f32[8,2,2,5,8192]{4,3,2,1,0:T(8,128)} reshape(f32[32,40960]{1,0:T(8,128)} %reduce-scatter.2.cloned.1.call-done) | data formatting | bytes 10485760 | tf_op jit(solution)/shard_map/reshape | solution.py:55
  281.9 7.8 %broadcast_multiply_fusion = f32[8,2,2,5,8192]{4,3,2,1,0:T(8,128)} fusion(f32[8,2,2,5,8192]{4,3,2,1,0:T(8,128)} %reshape.193, f32[8192]{0:T(1024)S(1)} %sqrt.3), kind=kLoop, calls=%fused_computation.2 | loop fusion | flops 1310720 | bytes 10518528 | tf_op jit(solution)/shard_map/mul | solution.py:56
  289.7 9.8 %copy.19 = f32[8,2,2,5,8192]{4,2,3,1,0:T(2,128)} copy(f32[8,2,2,5,8192]{4,3,2,1,0:T(8,128)} %broadcast_multiply_fusion) | data formatting | bytes 10485760
  (9 shorter events, 0.1 us)
Async XLA Ops:
  7.2 218.4 %reduce-scatter.2.cloned.1.call-start = ((), (), s32[]{:S(2)}) async-start(), calls=%async_computation.1 | async-start | bytes 26214400 | tf_op jit(solution)/shard_map/reduce_scatter | solution.py:49
  34.9 0.8 copy-start
Sparse Core Ops, SparseCore 0:
  35.1 190.4 reduce-scatter.1
where the time goes:
time: 308 us; the launch traced here: 306 us
  waiting for transfers between devices  190 us (62%)
  matrix products  39.8 us (13%)
  local copies, waits for them, and re-layouts  37.3 us (12%)
  blocking collectives  16.5 us (5%)
  between operations  14.1 us (5%)
  other arithmetic  8.87 us (3%)
    reduce_scatter x1, waiting for transfers between devices, on_device(): lax.psum_scatter(jnp.dot(rotation_multipliers, flat_snapshots, preferred_...  190 us
    dot_general x1, matrix products, gram_terms(): jnp.einsum('fam,fbm->fab', flat, flat, precision=lax.Precision.HIGHEST)  25.9 us
    unnamed x5, local copies, waits for them, and re-layouts  23.9 us
    psum x1, blocking collectives, on_device(): summed = lax.psum(gram_terms(spectra), ('px', 'py'))  16.5 us
    dot_general x1, matrix products, on_device(): jnp.dot(rotation_multipliers, flat_snapshots, preferred_element_type=jnp....  13.8 us
    reshape x2, local copies, waits for them, and re-layouts, on_device(): raw.reshape(RETAINED_MODES // groups, SEGMENT_NUMBER, 2, VARS, point_count)  13.2 us
    mul x1, other arithmetic, on_device(): spectra = raw * jnp.sqrt(quad_weights)  7.76 us
  transfers between devices with their start and end apart: 1, of which 1 were waited for; matrix products, arithmetic and copies ran while one was open for 0% of the time, Pallas kernels for 0%

commit v1 on v0

--- a/solution.py
+++ b/solution.py
@@ -1,8 +1,11 @@
+import functools
 import math
 
 import jax
 import jax.numpy as jnp
 from jax import lax
+from jax.experimental import pallas as pl
+from jax.experimental.pallas import tpu as pltpu
 from jax.sharding import PartitionSpec as P
 
 VARS = 5
@@ -10,6 +13,13 @@
 HOP = 128
 SEGMENT_NUMBER = 2
 RETAINED_MODES = 32
+
+MESH = pl.DeviceIdType.MESH
+HALF_NEIGHBOUR = (1, 2)
+POSITIONS = (0, 1, 3, 2)
+SENT_AT = ((1, 2), (2, 3))
+PASSED_AT = (3, 1)
+RECEIVED = ((0, 1), (1, 0))
 
 
 def make_rotation_multipliers(spectral_indices, temporal_locations):
@@ -37,7 +47,7 @@
     return jnp.stack([real_part, imag_part], axis=-1)
 
 
-def on_device(snapshots, quad_weights, spectral_indices):
+def plain_on_device(snapshots, quad_weights, spectral_indices):
     record_length = snapshots.shape[0]
     point_count = snapshots.shape[2]
     groups = lax.axis_size("ta")
@@ -60,9 +70,313 @@
     return (spectra, gram)
 
 
+def window_kernel(
+    pieces, width, tile, gram_scale,
+    snap_hbm, weight_ref, index_ref, out_hbm, gram_ref,
+    snap, twiddle, kept, root, send1, recv1, send2, recv2, out_buf, acc, gram_send, gram_recv,
+    load_sem, send1_sem, recv1_sem, send2_sem, recv2_sem, out_sem, gram_send_sem, gram_recv_sem,
+):
+    px, py, ta = lax.axis_index("px"), lax.axis_index("py"), lax.axis_index("ta")
+    npx, npy = lax.axis_size("px"), lax.axis_size("py")
+    variables, record, points = snap_hbm.shape
+    modes = out_hbm.shape[0]
+    unit = 2 * modes
+    steps = variables * pieces
+    slots = out_buf.shape[0]
+    neighbours = [jnp.bitwise_xor(ta, flip) for flip in HALF_NEIGHBOUR]
+
+    def load(variable):
+        return pltpu.make_async_copy(snap_hbm.at[variable], snap.at[variable], load_sem.at[variable])
+
+    for variable in range(variables):
+        load(variable).start()
+
+    peers = [
+        (i, j, lax.rem(px + i, npx), lax.rem(py + j, npy))
+        for i in range(npx) for j in range(npy) if i + j > 0
+    ]
+    barrier = pltpu.get_barrier_semaphore()
+    for neighbour in neighbours:
+        pl.semaphore_signal(barrier, inc=1, device_id=(px, py, neighbour), device_id_type=MESH)
+    for _, _, x, y in peers:
+        pl.semaphore_signal(barrier, inc=1, device_id=(x, y, ta), device_id_type=MESH)
+
+    def reaches(group, block):
+        first = group * record
+        return (first < block * HOP + BLK) & (first + record > block * HOP)
+
+    sublane = lax.broadcasted_iota(jnp.int32, (modes, record), 0)
+    moment = lax.broadcasted_iota(jnp.int32, (modes, record), 1) + ta * record
+    for position, flip in enumerate(POSITIONS):
+        owner = jnp.bitwise_xor(ta, flip)
+        bins = jnp.zeros((modes, record), jnp.int32)
+        for f in range(modes):
+            bins = jnp.where(sublane == f, index_ref[owner * modes + f], bins)
+        for block in range(SEGMENT_NUMBER):
+            shift = moment - block * HOP
+            inside = (shift >= 0) & (shift < BLK)
+            hann = 0.5 - 0.5 * jnp.cos((2.0 * math.pi / BLK) * shift.astype(jnp.float32))
+            hann = jnp.where(inside, hann, 0.0) / math.sqrt(3.0 * BLK / 8.0)
+            angle = (2.0 * math.pi / BLK) * jnp.bitwise_and(bins * shift, BLK - 1).astype(jnp.float32)
+            rows = jnp.concatenate([jnp.cos(angle) * hann, -jnp.sin(angle) * hann], axis=0)
+            at = (position * SEGMENT_NUMBER + block) * unit
+            twiddle[at:at + unit, :] = rows.astype(jnp.bfloat16)
+    root[...] = jnp.sqrt(weight_ref[...])
+    acc[...] = jnp.zeros_like(acc)
+
+    pl.semaphore_wait(barrier, len(neighbours) + len(peers))
+
+    def target(half):
+        return (px, py, neighbours[half])
+
+    def first_copy(half, k, block):
+        return pltpu.make_async_remote_copy(
+            src_ref=send1.at[half, k, block], dst_ref=recv1.at[half, k, block],
+            send_sem=send1_sem.at[half, k, block], recv_sem=recv1_sem.at[half, k, block],
+            device_id=target(half), device_id_type=MESH,
+        )
+
+    def second_copy(half, k):
+        return pltpu.make_async_remote_copy(
+            src_ref=send2.at[half, k], dst_ref=recv2.at[half, k],
+            send_sem=send2_sem.at[half, k], recv_sem=recv2_sem.at[half, k],
+            device_id=target(1 - half), device_id_type=MESH,
+        )
+
+    def columns(half, k, at):
+        start = lax.rem(k, pieces) * (2 * width) + half * width + at
+        return pl.ds(pl.multiple_of(start, 128), tile)
+
+    def transform(k):
+        variable = k // pieces
+
+        @pl.when(lax.rem(k, pieces) == 0)
+        def _():
+            load(variable).wait()
+
+        for half in range(2):
+            @pl.loop(0, width // tile)
+            def _(i):
+                at = pl.multiple_of(i * tile, tile)
+                here = pl.ds(at, tile)
+                product = jnp.dot(
+                    twiddle[...], snap[variable, :, columns(half, k, at)],
+                    preferred_element_type=jnp.float32,
+                )
+
+                def part(position, block):
+                    first = (position * SEGMENT_NUMBER + block) * unit
+                    return product[first:first + unit, :]
+
+                for block in range(SEGMENT_NUMBER):
+                    for place, position in enumerate(SENT_AT[half]):
+                        send1[half, k, block, place * unit:(place + 1) * unit, here] = part(
+                            position, block).astype(jnp.bfloat16)
+                    kept[half, k, block, 0:unit, here] = part(0, block)
+                    kept[half, k, block, unit:2 * unit, here] = part(PASSED_AT[half], block)
+
+            for block in range(SEGMENT_NUMBER):
+                @pl.when(reaches(ta, block))
+                def _():
+                    first_copy(half, k, block).start()
+
+    def pass_on(k):
+        for half in range(2):
+            own, other = RECEIVED[half]
+            for block in range(SEGMENT_NUMBER):
+                came = reaches(neighbours[half], block)
+
+                @pl.when(came)
+                def _():
+                    first_copy(half, k, block).wait_recv()
+
+                @pl.when(jnp.logical_not(came))
+                def _():
+                    recv1[half, k, block] = jnp.zeros(recv1.shape[3:], jnp.bfloat16)
+
+            @pl.loop(0, width // tile)
+            def _(i):
+                here = pl.ds(pl.multiple_of(i * tile, tile), tile)
+                for block in range(SEGMENT_NUMBER):
+                    arrived = recv1[half, k, block, other * unit:(other + 1) * unit, here]
+                    total = kept[half, k, block, unit:2 * unit, here] + arrived.astype(jnp.float32)
+                    send2[half, k, block * unit:(block + 1) * unit, here] = total.astype(jnp.bfloat16)
+
+            second_copy(half, k).start()
+
+    def write(half, k):
+        slot = lax.rem(k, slots)
+        start = pl.multiple_of(lax.rem(k, pieces) * (2 * width) + half * width, 128)
+        return pltpu.make_async_copy(
+            out_buf.at[slot, half],
+            out_hbm.at[:, :, k // pieces, :, pl.ds(start, width)],
+            out_sem.at[slot, half],
+        )
+
+    def finish(k):
+        slot = lax.rem(k, slots)
+        for half in range(2):
+            own, _ = RECEIVED[half]
+
+            @pl.when(k >= slots)
+            def _():
+                write(half, k - slots).wait()
+
+            second_copy(half, k).wait_recv()
+
+            @pl.loop(0, width // tile)
+            def _(i):
+                at = pl.multiple_of(i * tile, tile)
+                here = pl.ds(at, tile)
+                weight = root[:, columns(half, k, at)]
+                parts = []
+                for block in range(SEGMENT_NUMBER):
+                    first = recv1[half, k, block, own * unit:(own + 1) * unit, here]
+                    second = recv2[half, k, block * unit:(block + 1) * unit, here]
+                    total = kept[half, k, block, 0:unit, here] + (
+                        first.astype(jnp.float32) + second.astype(jnp.float32))
+                    total = total * weight
+                    parts.append((total[:modes], total[modes:]))
+                    out_buf[slot, half, :, block, 0, here] = total[:modes]
+                    out_buf[slot, half, :, block, 1, here] = total[modes:]
+                (r0, i0), (r1, i1) = parts
+                terms = (r0 * r0 + i0 * i0, r1 * r1 + i1 * i1, r0 * r1 + i0 * i1, r0 * i1 - i0 * r1)
+                for n, term in enumerate(terms):
+                    lanes = [term[:, c:c + 128] for c in range(0, tile, 128)]
+                    acc[n] += functools.reduce(jnp.add, lanes)
+
+            write(half, k).start()
+
+    ahead = min(2, steps)
+
+    @pl.loop(0, ahead)
+    def _(k):
+        transform(k)
+
+    @pl.loop(0, steps)
+    def _(k):
+        pass_on(k)
+
+        @pl.when(k + ahead < steps)
+        def _():
+            transform(k + ahead)
+
+        @pl.when(k >= 1)
+        def _():
+            finish(k - 1)
+
+    finish(steps - 1)
+
+    lane = lax.broadcasted_iota(jnp.int32, gram_send.shape, 1)
+    sums = jnp.zeros(gram_send.shape, jnp.float32)
+    for n in range(4):
+        sums = jnp.where(lane == n, jnp.sum(acc[n], axis=1, keepdims=True), sums)
+    gram_send[...] = sums
+
+    def gram_copy(n):
+        i, j, x, y = peers[n]
+        return pltpu.make_async_remote_copy(
+            src_ref=gram_send, dst_ref=gram_recv.at[n],
+            send_sem=gram_send_sem.at[n], recv_sem=gram_recv_sem.at[n],
+            device_id=(x, y, ta), device_id_type=MESH,
+        )
+
+    for n in range(len(peers)):
+        gram_copy(n).start()
+
+    @pl.loop(0, steps)
+    def _(k):
+        for half in range(2):
+            for block in range(SEGMENT_NUMBER):
+                @pl.when(reaches(ta, block))
+                def _():
+                    first_copy(half, k, block).wait_send()
+            second_copy(half, k).wait_send()
+
+    @pl.loop(max(steps - slots, 0), steps)
+    def _(k):
+        for half in range(2):
+            write(half, k).wait()
+
+    total = sums
+    for n in range(len(peers)):
+        gram_copy(n).wait()
+        total = total + gram_recv[n]
+    row = lax.broadcasted_iota(jnp.int32, (8, 128), 0)
+    lane = lax.broadcasted_iota(jnp.int32, (8, 128), 1)
+    pick = jnp.zeros((8, 128), jnp.float32)
+    for r, n, sign in ((0, 0, 1.0), (2, 2, 1.0), (3, 3, 1.0), (4, 2, 1.0), (5, 3, -1.0), (6, 1, 1.0)):
+        pick = jnp.where((row == r) & (lane == n), sign, pick)
+    gram_ref[...] = gram_scale * lax.dot_general(
+        pick, total, (((1,), (1,)), ((), ())),
+        precision=lax.Precision.HIGHEST, preferred_element_type=jnp.float32,
+    )
+
+
+def kernel_on_device(snapshots, quad_weights, spectral_indices):
+    record, variables, points = snapshots.shape
+    groups = lax.axis_size("ta")
+    npx, npy = lax.axis_size("px"), lax.axis_size("py")
+    modes = spectral_indices.shape[0] // groups
+    unit = 2 * modes
+    pieces = 2
+    width = points // (2 * pieces)
+    tile = min(512, width)
+    steps = variables * pieces
+    slots = 2
+    rows = groups * SEGMENT_NUMBER * unit
+    bf16, f32 = jnp.bfloat16, jnp.float32
+    peers = npx * npy - 1
+    spectra, gram = pl.pallas_call(
+        functools.partial(
+            window_kernel, pieces, width, tile, 1.0 / (points * npx * npy * variables)),
+        out_shape=(
+            jax.ShapeDtypeStruct((modes, SEGMENT_NUMBER, variables, 2, points), f32),
+            jax.ShapeDtypeStruct((SEGMENT_NUMBER * SEGMENT_NUMBER * 2, modes), f32),
+        ),
+        in_specs=[
+            pl.BlockSpec(memory_space=pl.ANY),
+            pl.BlockSpec(memory_space=pltpu.VMEM),
+            pl.BlockSpec(memory_space=pltpu.SMEM),
+        ],
+        out_specs=(
+            pl.BlockSpec(memory_space=pl.ANY),
+            pl.BlockSpec(memory_space=pltpu.VMEM),
+        ),
+        scratch_shapes=[
+            pltpu.VMEM((variables, record, points), bf16),
+            pltpu.VMEM((rows, record), bf16),
+            pltpu.VMEM((2, steps, SEGMENT_NUMBER, 2 * unit, width), f32),
+            pltpu.VMEM((1, points), f32),
+            pltpu.VMEM((2, steps, SEGMENT_NUMBER, 2 * unit, width), bf16),
+            pltpu.VMEM((2, steps, SEGMENT_NUMBER, 2 * unit, width), bf16),
+            pltpu.VMEM((2, steps, SEGMENT_NUMBER * unit, width), bf16),
+            pltpu.VMEM((2, steps, SEGMENT_NUMBER * unit, width), bf16),
+            pltpu.VMEM((slots, 2, modes, SEGMENT_NUMBER, 2, width), f32),
+            pltpu.VMEM((4, modes, 128), f32),
+            pltpu.VMEM((modes, 128), f32),
+            pltpu.VMEM((peers, modes, 128), f32),
+            pltpu.SemaphoreType.DMA((variables,)),
+            pltpu.SemaphoreType.DMA((2, steps, SEGMENT_NUMBER)),
+            pltpu.SemaphoreType.DMA((2, steps, SEGMENT_NUMBER)),
+            pltpu.SemaphoreType.DMA((2, steps)),
+            pltpu.SemaphoreType.DMA((2, steps)),
+            pltpu.SemaphoreType.DMA((slots, 2)),
+            pltpu.SemaphoreType.DMA((peers,)),
+            pltpu.SemaphoreType.DMA((peers,)),
+        ],
+        compiler_params=pltpu.CompilerParams(
+            collective_id=0, has_side_effects=True, vmem_limit_bytes=60 * 1024 * 1024),
+        name="window_transform",
+    )(snapshots.transpose(1, 0, 2), quad_weights.reshape(1, points), spectral_indices)
+    gram = gram.reshape(SEGMENT_NUMBER, SEGMENT_NUMBER, 2, modes)
+    return spectra.transpose(0, 1, 3, 2, 4), gram.transpose(3, 0, 1, 2)
+
+
 def solution(mesh):
+    square = mesh.shape["ta"] == len(POSITIONS)
     return jax.shard_map(
-        on_device,
+        kernel_on_device if square else plain_on_device,
         mesh=mesh,
         in_specs=(P("ta", None, ("px", "py")), P(("px", "py")), P()),
         out_specs=(P("ta", None, None, None, ("px", "py")), P("ta", None, None, None)),

time: 308 us -> 106 us (0.34)
  waiting for transfers between devices: 190 us -> 0 us
  Pallas kernels: 0 us -> 99.1 us
  matrix products: 39.8 us -> 0 us
  local copies, waits for them, and re-layouts: 37.3 us -> 6.08 us
  blocking collectives: 16.5 us -> 0 us
  between operations: 14.1 us -> 0.65 us
  other arithmetic: 8.87 us -> 0 us
    reduce_scatter x1 -> x0, waiting for transfers between devices: 190 us -> none  [on_device(): lax.psum_scatter(jnp.dot(rotation_multipliers, flat_snapshots, preferred_...]
    pallas_call x0 -> x1, Pallas kernels: none -> 99.1 us  [kernel_on_device(): pl.pallas_call(functools.partial(window_kernel, pieces, width, tile, 1.0...]
    dot_general x2 -> x0, matrix products: 39.8 us -> none  [the longest x1 25.9 us: gram_terms(): jnp.einsum('fam,fbm->fab', flat, flat, precision=lax.Precision.HIGHEST)]
    unnamed x5 -> x4, local copies, waits for them, and re-layouts: 23.9 us -> 6.08 us
    psum x1 -> x0, blocking collectives: 16.5 us -> none  [on_device(): summed = lax.psum(gram_terms(spectra), ('px', 'py'))]
    reshape x2 -> x0, local copies, waits for them, and re-layouts: 13.2 us -> none  [on_device(): raw.reshape(RETAINED_MODES // groups, SEGMENT_NUMBER, 2, VARS, point_count)]
    mul x2 -> x0, other arithmetic: 7.77 us -> none  [the longest x1 7.76 us: on_device(): spectra = raw * jnp.sqrt(quad_weights)]
  transfers between devices with their start and end apart: 1 -> 0, of which waited for: 1 -> 0; matrix products, arithmetic and copies ran while one was open for 0% -> 0% of each run, Pallas kernels for 0% -> 0%
where the time goes in v1:
time: 106 us
  Pallas kernels  99.1 us (93%)
  local copies, waits for them, and re-layouts  6.08 us (6%)
    pallas_call x1, Pallas kernels, kernel_on_device(): pl.pallas_call(functools.partial(window_kernel, pieces, width, tile, 1.0...  99.1 us
    unnamed x4, local copies, waits for them, and re-layouts  6.08 us

profile of v1, /device:TPU:0, one launch (start us, length us, event | category | flops | bytes accessed | tf_op | source)
XLA Modules:
  0.0 105.9 jit_solution(7086856455670895694)
XLA Ops:
  0.6 99.1 %window_transform.1 = (f32[8,2,5,2,8192]{4,3,2,1,0:T(2,128)}, f32[8,8]{1,0:T(8,128)}) custom-call(bf16[5,96,8192]{2,1,0:T(8,128)(2,1)} %bitcast.6, f32[1,8192]{1,0:T(1,128)} %bitcast.8, s32[32]{0:T(128)} %index_ref.1), custom_call_target="tpu_custom_call" | custom-call | tf_op jit(solution)/shard_map/window_transform/pallas_call | solution.py:330
  99.8 0.0 copy-start
  99.8 5.5 %copy.7 = f32[8,2,2,5,8192]{4,2,3,1,0:T(2,128)} copy(f32[8,2,2,5,8192]{4,2,3,1,0:T(2,128)} %bitcast.7) | data formatting | bytes 10485760
  105.3 0.0 copy-done
  105.3 0.6 copy.8
Async XLA Ops:
  99.8 5.5 %copy-start = (f32[8,8]{1,0:T(8,128)S(1)}, f32[8,8]{1,0:T(8,128)}, u32[]{:S(2)}) copy-start(f32[8,8]{1,0:T(8,128)} %get-tuple-element.5) | copy-start | bytes 772

commit v2 on v1

--- a/solution.py
+++ b/solution.py
@@ -72,24 +72,27 @@
 
 def window_kernel(
     pieces, width, tile, gram_scale,
-    snap_hbm, weight_ref, index_ref, out_hbm, gram_ref,
-    snap, twiddle, kept, root, send1, recv1, send2, recv2, out_buf, acc, gram_send, gram_recv,
-    load_sem, send1_sem, recv1_sem, send2_sem, recv2_sem, out_sem, gram_send_sem, gram_recv_sem,
+    snap_hbm, weight_hbm, index_hbm, out_ref, gram_ref,
+    snap, index_ref, weight_ref, twiddle, kept, root, send1, recv1, send2, recv2, acc, gram_send, gram_recv,
+    load_sem, index_sem, weight_sem, send1_sem, recv1_sem, send2_sem, recv2_sem, gram_send_sem, gram_recv_sem,
 ):
     px, py, ta = lax.axis_index("px"), lax.axis_index("py"), lax.axis_index("ta")
     npx, npy = lax.axis_size("px"), lax.axis_size("py")
     variables, record, points = snap_hbm.shape
-    modes = out_hbm.shape[0]
+    modes = out_ref.shape[0]
     unit = 2 * modes
     steps = variables * pieces
-    slots = out_buf.shape[0]
     neighbours = [jnp.bitwise_xor(ta, flip) for flip in HALF_NEIGHBOUR]
 
     def load(variable):
         return pltpu.make_async_copy(snap_hbm.at[variable], snap.at[variable], load_sem.at[variable])
 
+    index_copy = pltpu.make_async_copy(index_hbm, index_ref, index_sem)
+    weight_copy = pltpu.make_async_copy(weight_hbm, weight_ref, weight_sem)
+    index_copy.start()
     for variable in range(variables):
         load(variable).start()
+    weight_copy.start()
 
     peers = [
         (i, j, lax.rem(px + i, npx), lax.rem(py + j, npy))
@@ -107,21 +110,25 @@
 
     sublane = lax.broadcasted_iota(jnp.int32, (modes, record), 0)
     moment = lax.broadcasted_iota(jnp.int32, (modes, record), 1) + ta * record
+    shifts, windows = [], []
+    for block in range(SEGMENT_NUMBER):
+        shift = moment - block * HOP
+        inside = (shift >= 0) & (shift < BLK)
+        hann = 0.5 - 0.5 * jnp.cos((2.0 * math.pi / BLK) * shift.astype(jnp.float32))
+        shifts.append(shift)
+        windows.append(jnp.where(inside, hann, 0.0) / math.sqrt(3.0 * BLK / 8.0))
+    index_copy.wait()
     for position, flip in enumerate(POSITIONS):
         owner = jnp.bitwise_xor(ta, flip)
         bins = jnp.zeros((modes, record), jnp.int32)
         for f in range(modes):
             bins = jnp.where(sublane == f, index_ref[owner * modes + f], bins)
         for block in range(SEGMENT_NUMBER):
-            shift = moment - block * HOP
-            inside = (shift >= 0) & (shift < BLK)
-            hann = 0.5 - 0.5 * jnp.cos((2.0 * math.pi / BLK) * shift.astype(jnp.float32))
-            hann = jnp.where(inside, hann, 0.0) / math.sqrt(3.0 * BLK / 8.0)
+            shift, hann = shifts[block], windows[block]
             angle = (2.0 * math.pi / BLK) * jnp.bitwise_and(bins * shift, BLK - 1).astype(jnp.float32)
             rows = jnp.concatenate([jnp.cos(angle) * hann, -jnp.sin(angle) * hann], axis=0)
             at = (position * SEGMENT_NUMBER + block) * unit
             twiddle[at:at + unit, :] = rows.astype(jnp.bfloat16)
-    root[...] = jnp.sqrt(weight_ref[...])
     acc[...] = jnp.zeros_like(acc)
 
     pl.semaphore_wait(barrier, len(neighbours) + len(peers))
@@ -204,48 +211,43 @@
 
             second_copy(half, k).start()
 
-    def write(half, k):
-        slot = lax.rem(k, slots)
-        start = pl.multiple_of(lax.rem(k, pieces) * (2 * width) + half * width, 128)
-        return pltpu.make_async_copy(
-            out_buf.at[slot, half],
-            out_hbm.at[:, :, k // pieces, :, pl.ds(start, width)],
-            out_sem.at[slot, half],
-        )
+    def weighted(half, k, i):
+        own, _ = RECEIVED[half]
+        at = pl.multiple_of(i * tile, tile)
+        here = pl.ds(at, tile)
+        weight = root[:, columns(half, k, at)]
+        parts = []
+        for block in range(SEGMENT_NUMBER):
+            first = recv1[half, k, block, own * unit:(own + 1) * unit, here]
+            second = recv2[half, k, block * unit:(block + 1) * unit, here]
+            total = kept[half, k, block, 0:unit, here] + (
+                first.astype(jnp.float32) + second.astype(jnp.float32))
+            total = total * weight
+            parts.append((total[:modes], total[modes:]))
+        return parts
+
+    def add_terms(parts):
+        (r0, i0), (r1, i1) = parts
+        terms = (r0 * r0 + i0 * i0, r1 * r1 + i1 * i1, r0 * r1 + i0 * i1, r0 * i1 - i0 * r1)
+        for n, term in enumerate(terms):
+            lanes = [term[:, c:c + 128] for c in range(0, tile, 128)]
+            acc[n] += functools.reduce(jnp.add, lanes)
+
+    def store(half, k, i, parts):
+        here = columns(half, k, pl.multiple_of(i * tile, tile))
+        for block, both in enumerate(parts):
+            for c in range(2):
+                out_ref[:, block, k // pieces, c, here] = both[c]
 
     def finish(k):
-        slot = lax.rem(k, slots)
         for half in range(2):
-            own, _ = RECEIVED[half]
-
-            @pl.when(k >= slots)
-            def _():
-                write(half, k - slots).wait()
-
             second_copy(half, k).wait_recv()
 
             @pl.loop(0, width // tile)
             def _(i):
-                at = pl.multiple_of(i * tile, tile)
-                here = pl.ds(at, tile)
-                weight = root[:, columns(half, k, at)]
-                parts = []
-                for block in range(SEGMENT_NUMBER):
-                    first = recv1[half, k, block, own * unit:(own + 1) * unit, here]
-                    second = recv2[half, k, block * unit:(block + 1) * unit, here]
-                    total = kept[half, k, block, 0:unit, here] + (
-                        first.astype(jnp.float32) + second.astype(jnp.float32))
-                    total = total * weight
-                    parts.append((total[:modes], total[modes:]))
-                    out_buf[slot, half, :, block, 0, here] = total[:modes]
-                    out_buf[slot, half, :, block, 1, here] = total[modes:]
-                (r0, i0), (r1, i1) = parts
-                terms = (r0 * r0 + i0 * i0, r1 * r1 + i1 * i1, r0 * r1 + i0 * i1, r0 * i1 - i0 * r1)
-                for n, term in enumerate(terms):
-                    lanes = [term[:, c:c + 128] for c in range(0, tile, 128)]
-                    acc[n] += functools.reduce(jnp.add, lanes)
-
-            write(half, k).start()
+                parts = weighted(half, k, i)
+                add_terms(parts)
+                store(half, k, i, parts)
 
     ahead = min(2, steps)
 
@@ -253,6 +255,9 @@
     def _(k):
         transform(k)
 
+    weight_copy.wait()
+    root[...] = jnp.sqrt(weight_ref[...])
+
     @pl.loop(0, steps)
     def _(k):
         pass_on(k)
@@ -265,7 +270,12 @@
         def _():
             finish(k - 1)
 
-    finish(steps - 1)
+    for half in range(2):
+        second_copy(half, steps - 1).wait_recv()
+
+        @pl.loop(0, width // tile)
+        def _(i):
+            add_terms(weighted(half, steps - 1, i))
 
     lane = lax.broadcasted_iota(jnp.int32, gram_send.shape, 1)
     sums = jnp.zeros(gram_send.shape, jnp.float32)
@@ -283,6 +293,11 @@
 
     for n in range(len(peers)):
         gram_copy(n).start()
+
+    for half in range(2):
+        @pl.loop(0, width // tile)
+        def _(i):
+            store(half, steps - 1, i, weighted(half, steps - 1, i))
 
     @pl.loop(0, steps)
     def _(k):
@@ -292,11 +307,6 @@
                 def _():
                     first_copy(half, k, block).wait_send()
             second_copy(half, k).wait_send()
-
-    @pl.loop(max(steps - slots, 0), steps)
-    def _(k):
-        for half in range(2):
-            write(half, k).wait()
 
     total = sums
     for n in range(len(peers)):
@@ -319,11 +329,10 @@
     npx, npy = lax.axis_size("px"), lax.axis_size("py")
     modes = spectral_indices.shape[0] // groups
     unit = 2 * modes
-    pieces = 2
+    pieces = 4
     width = points // (2 * pieces)
-    tile = min(512, width)
+    tile = math.gcd(512, width)
     steps = variables * pieces
-    slots = 2
     rows = groups * SEGMENT_NUMBER * unit
     bf16, f32 = jnp.bfloat16, jnp.float32
     peers = npx * npy - 1
@@ -335,16 +344,18 @@
             jax.ShapeDtypeStruct((SEGMENT_NUMBER * SEGMENT_NUMBER * 2, modes), f32),
         ),
         in_specs=[
-            pl.BlockSpec(memory_space=pl.ANY),
-            pl.BlockSpec(memory_space=pltpu.VMEM),
-            pl.BlockSpec(memory_space=pltpu.SMEM),
+            pl.BlockSpec(memory_space=pltpu.HBM),
+            pl.BlockSpec(memory_space=pltpu.HBM),
+            pl.BlockSpec(memory_space=pltpu.HBM),
         ],
         out_specs=(
-            pl.BlockSpec(memory_space=pl.ANY),
+            pl.BlockSpec(memory_space=pltpu.VMEM),
             pl.BlockSpec(memory_space=pltpu.VMEM),
         ),
         scratch_shapes=[
             pltpu.VMEM((variables, record, points), bf16),
+            pltpu.SMEM(spectral_indices.shape, jnp.int32),
+            pltpu.VMEM((1, points), f32),
             pltpu.VMEM((rows, record), bf16),
             pltpu.VMEM((2, steps, SEGMENT_NUMBER, 2 * unit, width), f32),
             pltpu.VMEM((1, points), f32),
@@ -352,23 +363,26 @@
             pltpu.VMEM((2, steps, SEGMENT_NUMBER, 2 * unit, width), bf16),
             pltpu.VMEM((2, steps, SEGMENT_NUMBER * unit, width), bf16),
             pltpu.VMEM((2, steps, SEGMENT_NUMBER * unit, width), bf16),
-            pltpu.VMEM((slots, 2, modes, SEGMENT_NUMBER, 2, width), f32),
             pltpu.VMEM((4, modes, 128), f32),
             pltpu.VMEM((modes, 128), f32),
             pltpu.VMEM((peers, modes, 128), f32),
             pltpu.SemaphoreType.DMA((variables,)),
+            pltpu.SemaphoreType.DMA,
+            pltpu.SemaphoreType.DMA,
             pltpu.SemaphoreType.DMA((2, steps, SEGMENT_NUMBER)),
             pltpu.SemaphoreType.DMA((2, steps, SEGMENT_NUMBER)),
             pltpu.SemaphoreType.DMA((2, steps)),
             pltpu.SemaphoreType.DMA((2, steps)),
-            pltpu.SemaphoreType.DMA((slots, 2)),
             pltpu.SemaphoreType.DMA((peers,)),
             pltpu.SemaphoreType.DMA((peers,)),
         ],
         compiler_params=pltpu.CompilerParams(
-            collective_id=0, has_side_effects=True, vmem_limit_bytes=60 * 1024 * 1024),
+            collective_id=0, has_side_effects=True, vmem_limit_bytes=44 * 1024 * 1024),
         name="window_transform",
-    )(snapshots.transpose(1, 0, 2), quad_weights.reshape(1, points), spectral_indices)
+    )(*(
+        pltpu.with_memory_space_constraint(a, pltpu.HBM)
+        for a in (snapshots.transpose(1, 0, 2), quad_weights.reshape(1, points), spectral_indices)
+    ))
     gram = gram.reshape(SEGMENT_NUMBER, SEGMENT_NUMBER, 2, modes)
     return spectra.transpose(0, 1, 3, 2, 4), gram.transpose(3, 0, 1, 2)
 

time: 106 us -> 102 us (0.962)
  local copies, waits for them, and re-layouts: 6.08 us -> 2.95 us
  Pallas kernels: 99.1 us -> 97.9 us
    unnamed x4 -> x2, local copies, waits for them, and re-layouts: 6.08 us -> 2.95 us
    pallas_call x1, Pallas kernels: 99.1 us -> 97.9 us  [kernel_on_device(): pl.pallas_call(functools.partial(window_kernel, pieces, width, tile, 1.0...]
where the time goes in v2:
time: 102 us
  Pallas kernels  97.9 us (96%)
  local copies, waits for them, and re-layouts  2.95 us (3%)
    pallas_call x1, Pallas kernels, kernel_on_device(): pl.pallas_call(functools.partial(window_kernel, pieces, width, tile, 1.0...  97.9 us
    unnamed x2, local copies, waits for them, and re-layouts  2.95 us

profile of v2, /device:TPU:0, one launch (start us, length us, event | category | flops | bytes accessed | tf_op | source)
XLA Modules:
  0.0 101.5 jit_solution(8654286297287758396)
XLA Ops:
  0.6 97.9 %window_transform.1 = (f32[8,2,5,2,8192]{4,3,2,1,0:T(2,128)S(1)}, f32[8,8]{1,0:T(8,128)S(1)}) custom-call(bf16[5,96,8192]{2,1,0:T(8,128)(2,1)} %bitcast.8, f32[1,8192]{1,0:T(1,128)} %bitcast.9, s32[32]{0:T(128)} %index_hbm.1), custom_call_target="tpu_custom_call" | custom-call | tf_op jit(solution)/shard_map/window_transform/pallas_call | solution.py:339
  98.6 2.4 %copy.7 = f32[8,2,2,5,8192]{4,2,3,1,0:T(2,128)} copy(f32[8,2,2,5,8192]{4,2,3,1,0:T(2,128)S(1)} %bitcast.6) | data formatting | bytes 10485760
  100.9 0.6 copy.8

commit v3 on v2

--- a/solution.py
+++ b/solution.py
@@ -70,6 +70,18 @@
     return (spectra, gram)
 
 
+def sine_of_turn(m):
+    quarter = BLK // 4
+    r = jnp.bitwise_and(m + quarter, BLK - 1) - quarter
+    r = jnp.where(r > quarter, BLK // 2 - r, r)
+    x = r.astype(jnp.float32) * (2.0 * math.pi / BLK)
+    y = x * x
+    total = jnp.full_like(x, -1.0 / math.factorial(11))
+    for n in (9, 7, 5, 3, 1):
+        total = total * y + (1.0 if n % 4 == 1 else -1.0) / math.factorial(n)
+    return total * x
+
+
 def window_kernel(
     pieces, width, tile, gram_scale,
     snap_hbm, weight_hbm, index_hbm, out_ref, gram_ref,
@@ -114,7 +126,7 @@
     for block in range(SEGMENT_NUMBER):
         shift = moment - block * HOP
         inside = (shift >= 0) & (shift < BLK)
-        hann = 0.5 - 0.5 * jnp.cos((2.0 * math.pi / BLK) * shift.astype(jnp.float32))
+        hann = 0.5 - 0.5 * sine_of_turn(shift + BLK // 4)
         shifts.append(shift)
         windows.append(jnp.where(inside, hann, 0.0) / math.sqrt(3.0 * BLK / 8.0))
     index_copy.wait()
@@ -125,8 +137,9 @@
             bins = jnp.where(sublane == f, index_ref[owner * modes + f], bins)
         for block in range(SEGMENT_NUMBER):
             shift, hann = shifts[block], windows[block]
-            angle = (2.0 * math.pi / BLK) * jnp.bitwise_and(bins * shift, BLK - 1).astype(jnp.float32)
-            rows = jnp.concatenate([jnp.cos(angle) * hann, -jnp.sin(angle) * hann], axis=0)
+            phase = bins * shift
+            rows = jnp.concatenate(
+                [sine_of_turn(phase + BLK // 4) * hann, -sine_of_turn(phase) * hann], axis=0)
             at = (position * SEGMENT_NUMBER + block) * unit
             twiddle[at:at + unit, :] = rows.astype(jnp.bfloat16)
     acc[...] = jnp.zeros_like(acc)
@@ -329,7 +342,7 @@
     npx, npy = lax.axis_size("px"), lax.axis_size("py")
     modes = spectral_indices.shape[0] // groups
     unit = 2 * modes
-    pieces = 4
+    pieces = 2
     width = points // (2 * pieces)
     tile = math.gcd(512, width)
     steps = variables * pieces

time: 102 us -> 101 us (level)
  no operation moved by 1% of the time
where the time goes in v3:
time: 101 us
  Pallas kernels  97.6 us (97%)
  local copies, waits for them, and re-layouts  2.95 us (3%)
    pallas_call x1, Pallas kernels, kernel_on_device(): pl.pallas_call(functools.partial(window_kernel, pieces, width, tile, 1.0...  97.6 us
    unnamed x2, local copies, waits for them, and re-layouts  2.95 us

profile of v3, /device:TPU:0, one launch (start us, length us, event | category | flops | bytes accessed | tf_op | source)
XLA Modules:
  0.0 101.2 jit_solution(8260174741859135320)
XLA Ops:
  0.6 97.6 %window_transform.1 = (f32[8,2,5,2,8192]{4,3,2,1,0:T(2,128)S(1)}, f32[8,8]{1,0:T(8,128)S(1)}) custom-call(bf16[5,96,8192]{2,1,0:T(8,128)(2,1)} %bitcast.8, f32[1,8192]{1,0:T(1,128)} %bitcast.9, s32[32]{0:T(128)} %index_hbm.1), custom_call_target="tpu_custom_call" | custom-call | tf_op jit(solution)/shard_map/window_transform/pallas_call | solution.py:352
  98.3 2.4 %copy.7 = f32[8,2,2,5,8192]{4,2,3,1,0:T(2,128)} copy(f32[8,2,2,5,8192]{4,2,3,1,0:T(2,128)S(1)} %bitcast.6) | data formatting | bytes 10485760
  100.6 0.6 copy.8
